TPU v7x, 32 devices: a whole 2x2x4 slice. The times are simulated.
32 devices in a mesh: rows: 8 (over z, x), cols: 4 (over y, core).
Axes of the slice: x: 2, y: 2, z: 4, core: 2. Of those that a mesh axis runs over, the one named last changes fastest.
Arguments:
- vectors: bfloat16 [1024, 32768], P(None, 'rows'), may hold values from -0.4 to 0.4
- integrals: bfloat16 [2, 256, 32768], P(None, 'cols', 'rows'), may hold values from -8 to 72
- pivots: int32 [2, 256], replicated, may hold values from 0 to 32767, as said below
Outputs:
- new_vectors: float32 [2, 256, 32768], P(None, 'cols', 'rows')
Inputs may be any that keep to these rules, and one draw needn't show every extreme that they name: The 2 x 256 entries are distinct shell-pair rows. In each panel the rows of one index of rows (an aligned block of 4096) hold at most 64 pivots, and some block holds exactly 64.
All inputs are finite; a program needn't handle non-finite values.
Results may differ from a plain program's by a relative error of at most 0.00036.
Values may be sent and summed in bfloat16 or wider, within the bound.
No kernel may reach another device: no remote copies, remote signals or barrier semaphores. Data moves between devices by JAX's collectives and lax.ppermute only.
A program may use at most 64 MiB of HBM per device.

v0:
```python
import jax
import jax.numpy as jnp
from jax import lax
from jax.sharding import PartitionSpec as P

PW = 256
PANELS = 2


def select_matrix(row_count, targets):
    return (jnp.arange(row_count, dtype=jnp.int32)[:, None] == targets[None, :]).astype(
        jnp.bfloat16
    )


def transposed_product(left, right):
    return lax.dot_general(
        left, right, (((0,), (0,)), ((), ())), preferred_element_type=jnp.float32
    )


def solve_block(lower_factor, residual):
    return jax.scipy.linalg.solve_triangular(lower_factor, residual, lower=True)


def per_device(vectors, integrals, pivots):
    row_count = vectors.shape[1]
    block_cols = integrals.shape[1]
    owners = lax.axis_size("rows")
    owner_index = lax.axis_index("rows")
    owner_start = owner_index * row_count
    col_start = lax.axis_index("cols") * block_cols
    factors = [vectors]
    results = []
    for panel in range(PANELS):
        pivot_row = pivots[panel]
        local_targets = pivot_row - owner_start
        slot_count = 2 * PW // owners
        owner_of = pivot_row // row_count
        order = jnp.arange(PW, dtype=jnp.int32)
        earlier = (owner_of[None, :] == owner_of[:, None]) & (order[None, :] < order[:, None])
        slot_rank = jnp.sum(earlier.astype(jnp.int32), axis=1)
        mine = owner_of == owner_index
        slot_pick = (
            (slot_rank[:, None] == jnp.arange(slot_count, dtype=jnp.int32)[None, :]) & mine[:, None]
        ).astype(jnp.bfloat16)
        slot_select = jnp.dot(
            select_matrix(row_count, local_targets), slot_pick, preferred_element_type=jnp.float32
        ).astype(jnp.bfloat16)
        sending = jnp.concatenate(
            [
                jnp.dot(factor, slot_select, preferred_element_type=jnp.float32)
                for factor in factors
            ],
            axis=0,
        ).astype(jnp.bfloat16)
        targets = lax.dynamic_slice_in_dim(owner_of * slot_count + slot_rank, col_start, block_cols)
        receive_pick = select_matrix(owners * slot_count, targets)
        picked = jnp.dot(
            lax.all_gather(sending, "rows", axis=1, tiled=True),
            receive_pick,
            preferred_element_type=jnp.float32,
        ).astype(jnp.bfloat16)
        residual = integrals[panel].astype(jnp.float32)
        offset = 0
        for factor in factors:
            residual = residual - transposed_product(
                picked[offset : offset + factor.shape[0]], factor
            )
            offset = offset + factor.shape[0]
        every_pivot = select_matrix(row_count, local_targets).astype(jnp.float32)
        contribution = jnp.dot(residual, every_pivot, precision=lax.Precision.HIGHEST)
        placed = lax.dynamic_update_slice(
            jnp.zeros((PW, PW), jnp.float32), contribution, (col_start, 0)
        )
        block = lax.psum(placed, ("rows", "cols"))
        lower_factor = jnp.linalg.cholesky(0.5 * (block + block.T))
        whole = lax.all_gather(residual, "cols", axis=0, tiled=True)
        solved = solve_block(lower_factor, whole)
        fresh = lax.dynamic_slice_in_dim(solved, col_start, block_cols, 0)
        if panel + 1 < PANELS:
            factors.append(solved.astype(jnp.bfloat16))
        results.append(fresh)
    return jnp.stack(results)


def solution(mesh):
    placed = (P(None, "rows"), P(None, "cols", "rows"), P())
    return jax.shard_map(
        per_device, mesh=mesh, in_specs=placed, out_specs=P(None, "cols", "rows"), check_vma=False
    )
```

profile of v0, /device:TPU:0, one launch (start us, length us, event | category | flops | bytes accessed | tf_op | source)
XLA Modules:
  0.0 519.9 jit_solution(4560592978291593466)
XLA Ops:
  7.5 7.5 %fusion.14 = bf16[1024,64]{0,1:T(8,128)(2,1)} fusion(bf16[1024,4096]{1,0:T(8,128)(2,1)} %param.6, s32[256]{0:T(256)S(1)} %bitcast.98, s32[256]{0:T(256)S(1)} %convert_reduce_fusion.1, pred[256]{0:T(512)(128)(4,1)S(1)} %get-tuple-element.65), kind=kOutput, calls=%fused_computation.36 | convolution fusion | flops 672497664 | bytes 8521984 | tf_op jit(solution)/shard_map/dot_general | solution.py:52
  15.2 43.0 %all-gather.5.cloned.1.call-done = bf16[1024,512]{0,1:T(8,128)(2,1)} async-done(((bf16[1024,64]{0,1:T(8,128)(2,1)}), bf16[1024,512]{0,1:T(8,128)(2,1)}) %all-gather.5.cloned.1.call-update) | async-done | bytes 1048592 | tf_op jit(solution)/shard_map/all_gather | solution.py:60
  58.2 5.9 %convolution_subtract_fusion.4 = f32[64,4096]{1,0:T(8,128)S(1)} fusion(bf16[1024,4096]{1,0:T(8,128)(2,1)} %param.6, bf16[1024,512]{0,1:T(8,128)(2,1)} %all-gather.5.cloned.1.call-done, bf16[2,64,4096]{2,1,0:T(8,128)(2,1)S(1)} %copy-done.6, s32[64]{0:T(128)S(1)} %dynamic_slice.12), kind=kOutput, calls=%fused_computation.12 | convolution fusion | flops 604602368 | bytes 11010304 | tf_op jit(solution)/shard_map/dot_general | solution.py:17
  64.1 1.7 fusion.15
  68.7 6.1 %fusion.13 = bf16[1024,64]{0,1:T(8,128)(2,1)S(1)} fusion(bf16[4096,64]{0,1:T(8,128)(2,1)S(1)} %convolution_convert_fusion.1, bf16[1024,4096]{1,0:T(8,128)(2,1)} %param.6), kind=kOutput, calls=%fused_computation.35 | convolution fusion | flops 536936448 | bytes 9043968 | tf_op jit(solution)/shard_map/dot_general | solution.py:52
  74.7 117.2 %all-reduce.4.cloned.1.call-done = f32[256,256]{1,0:T(8,128)} async-done(((f32[256,256]{1,0:T(8,128)}), f32[256,256]{1,0:T(8,128)}) %all-reduce.4.cloned.1.call-update) | async-done | bytes 262160 | tf_op jit(solution)/shard_map/psum | solution.py:76
  194.2 11.7 %cholesky.130 = f32[128,128]{1,0:T(8,128)S(1)} custom-call(f32[128,128]{1,0:T(8,128)S(1)} %cholesky.194), custom_call_target="Cholesky" | custom-call | tf_op jit(solution)/shard_map/jit(cholesky)/cholesky | solution.py:77
  206.0 9.8 %custom-call.13 = f32[1,128,128]{1,2,0:T(8,128)S(1)} custom-call(f32[1,128,128]{2,1,0:T(8,128)S(1)} %get-tuple-element.54), custom_call_target="InvertDiagBlocksLowerTriangular" | custom-call | tf_op jit(solution)/shard_map/jit(cholesky)/cholesky | solution.py:77
  216.3 11.9 %cholesky.147 = f32[128,128]{1,0:T(8,128)S(1)} custom-call(f32[128,128]{1,0:T(8,128)S(1)} %convolution_subtract_fusion.6), custom_call_target="Cholesky" | custom-call | tf_op jit(solution)/shard_map/jit(cholesky)/cholesky | solution.py:77
  231.0 4.1 while.4
  231.7 1.4 bitcast_dynamic-update-slice_fusion.4
  233.7 1.4 bitcast_dynamic-update-slice_fusion.4
  235.1 19.7 %custom-call.14 = f32[2,128,128]{1,2,0:T(8,128)S(1)} custom-call(f32[2,128,128]{2,1,0:T(8,128)S(1)} %get-tuple-element.21), custom_call_target="InvertDiagBlocksLowerTriangular" | custom-call | tf_op jit(solution)/shard_map/jit(_solve_triangular)/triangular_solve | solution.py:23
  254.8 3.6 fusion.5
  258.5 1.9 convolution_subtract_fusion.1
  260.4 1.9 fusion.42
  264.6 40.9 %all-gather.9.cloned.1.call-done = bf16[1280,512]{0,1:T(8,128)(2,1)} async-done(((bf16[1280,64]{0,1:T(8,128)(2,1)}), bf16[1280,512]{0,1:T(8,128)(2,1)}) %all-gather.9.cloned.1.call-update) | async-done | bytes 1310736 | tf_op jit(solution)/shard_map/all_gather | solution.py:60
  305.5 1.7 convolution_convert_fusion.2
  307.2 5.1 convolution_subtract_fusion.3
  312.9 1.7 fusion.16
  316.0 124.8 %all-reduce.6.cloned.1.call-done = f32[256,256]{1,0:T(8,128)} async-done(((f32[256,256]{1,0:T(8,128)}), f32[256,256]{1,0:T(8,128)}) %all-reduce.6.cloned.1.call-update) | async-done | bytes 262160 | tf_op jit(solution)/shard_map/psum | solution.py:76
  443.3 11.7 %cholesky.164 = f32[128,128]{1,0:T(8,128)S(1)} custom-call(f32[128,128]{1,0:T(8,128)S(1)} %cholesky.197), custom_call_target="Cholesky" | custom-call | tf_op jit(solution)/shard_map/jit(cholesky)/cholesky | solution.py:77
  455.0 9.8 %custom-call.15 = f32[1,128,128]{1,2,0:T(8,128)S(1)} custom-call(f32[1,128,128]{2,1,0:T(8,128)S(1)} %get-tuple-element.50), custom_call_target="InvertDiagBlocksLowerTriangular" | custom-call | tf_op jit(solution)/shard_map/jit(cholesky)/cholesky | solution.py:77
  465.4 11.7 %cholesky.181 = f32[128,128]{1,0:T(8,128)S(1)} custom-call(f32[128,128]{1,0:T(8,128)S(1)} %convolution_subtract_fusion.5), custom_call_target="Cholesky" | custom-call | tf_op jit(solution)/shard_map/jit(cholesky)/cholesky | solution.py:77
  479.7 4.1 while.5
  480.5 1.4 bitcast_dynamic-update-slice_fusion.5
  482.5 1.4 bitcast_dynamic-update-slice_fusion.5
  483.9 19.7 %custom-call.16 = f32[2,128,128]{1,2,0:T(8,128)S(1)} custom-call(f32[2,128,128]{2,1,0:T(8,128)S(1)} %get-tuple-element.22), custom_call_target="InvertDiagBlocksLowerTriangular" | custom-call | tf_op jit(solution)/shard_map/jit(_solve_triangular)/triangular_solve | solution.py:23
  503.6 3.6 fusion.3
  507.2 1.9 convolution_subtract_fusion
  509.2 1.9 fusion.38
  511.3 1.5 pad_maximum_fusion.1
  (90 shorter events, 19.4 us)
Async XLA Ops:
  6.5 51.7 %all-gather.5.cloned.1.call-start = ((), (), s32[]{:S(2)}) async-start(), calls=%async_computation | async-start | bytes 1179648 | tf_op jit(solution)/shard_map/all_gather | solution.py:60
  7.5 50.7 %copy-start.6 = (bf16[2,64,4096]{2,1,0:T(8,128)(2,1)S(1)}, bf16[2,64,4096]{2,1,0:T(8,128)(2,1)}, u32[]{:S(2)}) copy-start(bf16[2,64,4096]{2,1,0:T(8,128)(2,1)} %param.7) | copy-start | bytes 3145732
  15.0 176.9 %all-reduce.4.cloned.1.call-start = ((), (), s32[]{:S(2)}) async-start(), calls=%async_computation.1 | async-start | bytes 524288 | tf_op jit(solution)/shard_map/psum | solution.py:76
  64.1 2.5 copy-start.5
  65.8 0.7 copy-start.8
  66.5 188.3 %all-gather.7.cloned.1.call-start = ((), (), s32[]{:S(2)}) async-start(), calls=%async_computation.2 | async-start | bytes 5242880 | tf_op jit(solution)/shard_map/all_gather | solution.py:78
  67.3 238.2 %all-gather.9.cloned.1.call-start = ((), (), s32[]{:S(2)}) async-start(), calls=%async_computation.3 | async-start | bytes 1474560 | tf_op jit(solution)/shard_map/all_gather | solution.py:60
  254.8 3.7 copy-start.2
  262.4 1.3 copy-start
  263.7 43.5 %copy-start.7 = (bf16[2,64,4096]{2,1,0:T(8,128)(2,1)S(1)}, bf16[2,64,4096]{2,1,0:T(8,128)(2,1)}, u32[]{:S(2)}) copy-start(bf16[2,64,4096]{2,1,0:T(8,128)(2,1)} %param.7) | copy-start | bytes 3145732
  264.4 176.4 %all-reduce.6.cloned.1.call-start = ((), (), s32[]{:S(2)}) async-start(), calls=%async_computation.4 | async-start | bytes 524288 | tf_op jit(solution)/shard_map/psum | solution.py:76
  307.2 5.2 copy-start.1
  312.9 2.9 copy-start.4
  314.6 0.7 copy-start.9
  315.3 188.3 %all-gather.11.cloned.1.call-start = ((), (), s32[]{:S(2)}) async-start(), calls=%async_computation.5 | async-start | bytes 5242880 | tf_op jit(solution)/shard_map/all_gather | solution.py:78
  503.6 3.7 copy-start.3
Sparse Core Ops, SparseCore 0:
  15.2 42.9 all-gather.4
  66.6 125.2 all-reduce.3
  193.5 33.7 all-gather.6
  264.5 40.8 all-gather.8
  315.4 125.3 all-reduce.5
  442.3 33.6 all-gather.10
where the time goes:
time: 525 us; the launch traced here: 520 us
  waiting for transfers between devices  327 us (62%)
  other arithmetic  115 us (22%)
  matrix products  47.8 us (9%)
  between operations  16.7 us (3%)
  local copies, waits for them, and re-layouts  12.8 us (2%)
    psum x2, waiting for transfers between devices, per_device(): block = lax.psum(placed, ('rows', 'cols'))  242 us
    all_gather x2, waiting for transfers between devices, per_device(): lax.all_gather(sending, 'rows', axis=1, tiled=True)  83.9 us
    another operation x14, other arithmetic, per_device(): lower_factor = jnp.linalg.cholesky(0.5 * (block + block.T))  69.4 us
    another operation x5, other arithmetic, solve_block(): return jax.scipy.linalg.solve_triangular(lower_factor, residual, lower=True)  39.4 us
    another operation x6, matrix products, solve_block(): return jax.scipy.linalg.solve_triangular(lower_factor, residual, lower=True)  15 us
    dot_general x3, matrix products, per_device(): jnp.dot(factor, slot_select, preferred_element_type=jnp.float32)  14.4 us
    dot_general x3, matrix products, transposed_product(): lax.dot_general(left, right, (((0,), (0,)), ((), ())), preferred_element_...  11.5 us
  transfers between devices with their start and end apart: 6, of which 4 were waited for; matrix products, arithmetic and copies ran while one was open for 25% of the time, Pallas kernels for 0%

commit v1 on v0

--- a/solution.py
+++ b/solution.py
@@ -73,7 +73,9 @@
         placed = lax.dynamic_update_slice(
             jnp.zeros((PW, PW), jnp.float32), contribution, (col_start, 0)
         )
-        block = lax.psum(placed, ("rows", "cols"))
+        block = placed
+        for mesh_axis in ("rows", "cols"):
+            block = lax.psum(block, mesh_axis)
         lower_factor = jnp.linalg.cholesky(0.5 * (block + block.T))
         whole = lax.all_gather(residual, "cols", axis=0, tiled=True)
         solved = solve_block(lower_factor, whole)

time: 525 us -> 483 us (0.920)
  waiting for transfers between devices: 327 us -> 284 us
    psum x2 -> x4, waiting for transfers between devices: 242 us -> 199 us  [per_device(): block = lax.psum(block, mesh_axis)]
  transfers between devices with their start and end apart: 6 -> 8, of which waited for: 4 -> 6; matrix products, arithmetic and copies ran while one was open for 25% -> 27% of each run, Pallas kernels for 0% -> 0%
where the time goes in v1:
time: 483 us; the launch traced here: 477 us
  waiting for transfers between devices  284 us (59%)
  other arithmetic  115 us (24%)
  matrix products  47.8 us (10%)
  between operations  16.7 us (3%)
  local copies, waits for them, and re-layouts  12.8 us (3%)
    psum x4, waiting for transfers between devices, per_device(): block = lax.psum(block, mesh_axis)  199 us
    all_gather x2, waiting for transfers between devices, per_device(): lax.all_gather(sending, 'rows', axis=1, tiled=True)  84.8 us
    another operation x14, other arithmetic, per_device(): lower_factor = jnp.linalg.cholesky(0.5 * (block + block.T))  69.5 us
    another operation x5, other arithmetic, solve_block(): return jax.scipy.linalg.solve_triangular(lower_factor, residual, lower=True)  39.4 us
    another operation x6, matrix products, solve_block(): return jax.scipy.linalg.solve_triangular(lower_factor, residual, lower=True)  15 us
    dot_general x3, matrix products, per_device(): jnp.dot(factor, slot_select, preferred_element_type=jnp.float32)  14.3 us
    dot_general x3, matrix products, transposed_product(): lax.dot_general(left, right, (((0,), (0,)), ((), ())), preferred_element_...  11.5 us
  transfers between devices with their start and end apart: 8, of which 6 were waited for; matrix products, arithmetic and copies ran while one was open for 27% of the time, Pallas kernels for 0%

profile of v1, /device:TPU:0, one launch (start us, length us, event | category | flops | bytes accessed | tf_op | source)
XLA Modules:
  0.0 477.5 jit_solution(16614069924963970774)
XLA Ops:
  7.5 7.5 %fusion.14 = bf16[1024,64]{0,1:T(8,128)(2,1)} fusion(bf16[1024,4096]{1,0:T(8,128)(2,1)} %param.6, s32[256]{0:T(256)S(1)} %bitcast.98, s32[256]{0:T(256)S(1)} %convert_reduce_fusion.1, pred[256]{0:T(512)(128)(4,1)S(1)} %get-tuple-element.65), kind=kOutput, calls=%fused_computation.36 | convolution fusion | flops 672497664 | bytes 8521984 | tf_op jit(solution)/shard_map/dot_general | solution.py:52
  15.2 43.0 %all-gather.5.cloned.1.call-done = bf16[1024,512]{0,1:T(8,128)(2,1)} async-done(((bf16[1024,64]{0,1:T(8,128)(2,1)}), bf16[1024,512]{0,1:T(8,128)(2,1)}) %all-gather.5.cloned.1.call-update) | async-done | bytes 1048592 | tf_op jit(solution)/shard_map/all_gather | solution.py:60
  58.2 5.9 %convolution_subtract_fusion.4 = f32[64,4096]{1,0:T(8,128)S(1)} fusion(bf16[1024,4096]{1,0:T(8,128)(2,1)} %param.6, bf16[1024,512]{0,1:T(8,128)(2,1)} %all-gather.5.cloned.1.call-done, bf16[2,64,4096]{2,1,0:T(8,128)(2,1)S(1)} %copy-done.6, s32[64]{0:T(128)S(1)} %dynamic_slice.12), kind=kOutput, calls=%fused_computation.12 | convolution fusion | flops 604602368 | bytes 11010304 | tf_op jit(solution)/shard_map/dot_general | solution.py:17
  64.1 1.7 fusion.15
  66.5 69.9 %all-reduce.6.cloned.1.call-done = f32[256,256]{1,0:T(8,128)} async-done(((f32[256,256]{1,0:T(8,128)}), f32[256,256]{1,0:T(8,128)}) %all-reduce.6.cloned.1.call-update) | async-done | bytes 262160 | tf_op jit(solution)/shard_map/psum | solution.py:78
  138.4 6.0 %fusion.13 = bf16[1024,64]{0,1:T(8,128)(2,1)S(1)} fusion(bf16[4096,64]{0,1:T(8,128)(2,1)S(1)} %convolution_convert_fusion.1, bf16[1024,4096]{1,0:T(8,128)(2,1)} %param.6), kind=kOutput, calls=%fused_computation.35 | convolution fusion | flops 536936448 | bytes 9043968 | tf_op jit(solution)/shard_map/dot_general | solution.py:52
  144.4 25.9 %all-reduce.8.cloned.1.call-done = f32[256,256]{1,0:T(8,128)} async-done(((f32[256,256]{1,0:T(8,128)}), f32[256,256]{1,0:T(8,128)}) %all-reduce.8.cloned.1.call-update) | async-done | bytes 262160 | tf_op jit(solution)/shard_map/psum | solution.py:78
  172.6 11.7 %cholesky.130 = f32[128,128]{1,0:T(8,128)S(1)} custom-call(f32[128,128]{1,0:T(8,128)S(1)} %cholesky.194), custom_call_target="Cholesky" | custom-call | tf_op jit(solution)/shard_map/jit(cholesky)/cholesky | solution.py:79
  184.3 9.8 %custom-call.13 = f32[1,128,128]{1,2,0:T(8,128)S(1)} custom-call(f32[1,128,128]{2,1,0:T(8,128)S(1)} %get-tuple-element.54), custom_call_target="InvertDiagBlocksLowerTriangular" | custom-call | tf_op jit(solution)/shard_map/jit(cholesky)/cholesky | solution.py:79
  194.7 11.9 %cholesky.147 = f32[128,128]{1,0:T(8,128)S(1)} custom-call(f32[128,128]{1,0:T(8,128)S(1)} %convolution_subtract_fusion.6), custom_call_target="Cholesky" | custom-call | tf_op jit(solution)/shard_map/jit(cholesky)/cholesky | solution.py:79
  209.4 4.1 while.4
  210.1 1.4 bitcast_dynamic-update-slice_fusion.4
  212.1 1.4 bitcast_dynamic-update-slice_fusion.4
  213.5 19.7 %custom-call.14 = f32[2,128,128]{1,2,0:T(8,128)S(1)} custom-call(f32[2,128,128]{2,1,0:T(8,128)S(1)} %get-tuple-element.21), custom_call_target="InvertDiagBlocksLowerTriangular" | custom-call | tf_op jit(solution)/shard_map/jit(_solve_triangular)/triangular_solve | solution.py:23
  233.2 3.6 fusion.5
  236.9 1.9 convolution_subtract_fusion.1
  238.8 1.9 fusion.42
  243.0 41.8 %all-gather.9.cloned.1.call-done = bf16[1280,512]{0,1:T(8,128)(2,1)} async-done(((bf16[1280,64]{0,1:T(8,128)(2,1)}), bf16[1280,512]{0,1:T(8,128)(2,1)}) %all-gather.9.cloned.1.call-update) | async-done | bytes 1310736 | tf_op jit(solution)/shard_map/all_gather | solution.py:60
  284.8 1.7 convolution_convert_fusion.2
  286.5 5.1 %convolution_subtract_fusion.3 = f32[64,4096]{1,0:T(8,128)S(1)} fusion(bf16[1024,4096]{1,0:T(8,128)(2,1)} %param.6, bf16[2,64,4096]{2,1,0:T(8,128)(2,1)S(1)} %copy-done.7, bf16[1280,64]{0,1:T(8,128)(2,1)S(1)} %convolution_convert_fusion.2), kind=kOutput, calls=%fused_computation.11 | convolution fusion | flops 537395200 | bytes 10092544 | tf_op jit(solution)/shard_map/dot_general | solution.py:17
  292.2 1.7 fusion.16
  294.7 69.9 %all-reduce.10.cloned.1.call-done = f32[256,256]{1,0:T(8,128)} async-done(((f32[256,256]{1,0:T(8,128)}), f32[256,256]{1,0:T(8,128)}) %all-reduce.10.cloned.1.call-update) | async-done | bytes 262160 | tf_op jit(solution)/shard_map/psum | solution.py:78
  365.5 32.9 %all-reduce.12.cloned.1.call-done = f32[256,256]{1,0:T(8,128)} async-done(((f32[256,256]{1,0:T(8,128)}), f32[256,256]{1,0:T(8,128)}) %all-reduce.12.cloned.1.call-update) | async-done | bytes 262160 | tf_op jit(solution)/shard_map/psum | solution.py:78
  400.9 11.7 %cholesky.164 = f32[128,128]{1,0:T(8,128)S(1)} custom-call(f32[128,128]{1,0:T(8,128)S(1)} %cholesky.197), custom_call_target="Cholesky" | custom-call | tf_op jit(solution)/shard_map/jit(cholesky)/cholesky | solution.py:79
  412.6 9.8 %custom-call.15 = f32[1,128,128]{1,2,0:T(8,128)S(1)} custom-call(f32[1,128,128]{2,1,0:T(8,128)S(1)} %get-tuple-element.50), custom_call_target="InvertDiagBlocksLowerTriangular" | custom-call | tf_op jit(solution)/shard_map/jit(cholesky)/cholesky | solution.py:79
  422.9 11.7 %cholesky.181 = f32[128,128]{1,0:T(8,128)S(1)} custom-call(f32[128,128]{1,0:T(8,128)S(1)} %convolution_subtract_fusion.5), custom_call_target="Cholesky" | custom-call | tf_op jit(solution)/shard_map/jit(cholesky)/cholesky | solution.py:79
  437.3 4.1 while.5
  441.4 19.7 %custom-call.16 = f32[2,128,128]{1,2,0:T(8,128)S(1)} custom-call(f32[2,128,128]{2,1,0:T(8,128)S(1)} %get-tuple-element.22), custom_call_target="InvertDiagBlocksLowerTriangular" | custom-call | tf_op jit(solution)/shard_map/jit(_solve_triangular)/triangular_solve | solution.py:23
  461.2 3.6 fusion.3
  464.8 1.9 convolution_subtract_fusion
  466.7 1.9 fusion.38
  468.9 1.5 pad_maximum_fusion.1
  (96 shorter events, 22.2 us)
Async XLA Ops:
  6.5 51.7 %all-gather.5.cloned.1.call-start = ((), (), s32[]{:S(2)}) async-start(), calls=%async_computation | async-start | bytes 1179648 | tf_op jit(solution)/shard_map/all_gather | solution.py:60
  7.5 50.7 %copy-start.6 = (bf16[2,64,4096]{2,1,0:T(8,128)(2,1)S(1)}, bf16[2,64,4096]{2,1,0:T(8,128)(2,1)}, u32[]{:S(2)}) copy-start(bf16[2,64,4096]{2,1,0:T(8,128)(2,1)} %param.7) | copy-start | bytes 3145732
  15.0 121.4 %all-reduce.6.cloned.1.call-start = ((), (), s32[]{:S(2)}) async-start(), calls=%async_computation.1 | async-start | bytes 524288 | tf_op jit(solution)/shard_map/psum | solution.py:78
  64.1 72.4 %copy-start.5 = (f32[64,4096]{1,0:T(8,128)}, f32[64,4096]{1,0:T(8,128)S(1)}, u32[]{:S(2)}) copy-start(f32[64,4096]{1,0:T(8,128)S(1)} %convolution_subtract_fusion.4) | copy-start | bytes 3145732
  65.8 0.7 copy-start.8
  66.5 103.8 %all-reduce.8.cloned.1.call-start = ((), (), s32[]{:S(2)}) async-start(), calls=%async_computation.2 | async-start | bytes 524288 | tf_op jit(solution)/shard_map/psum | solution.py:78
  136.4 96.8 %all-gather.7.cloned.1.call-start = ((), (), s32[]{:S(2)}) async-start(), calls=%async_computation.3 | async-start | bytes 5242880 | tf_op jit(solution)/shard_map/all_gather | solution.py:80
  137.0 147.8 %all-gather.9.cloned.1.call-start = ((), (), s32[]{:S(2)}) async-start(), calls=%async_computation.4 | async-start | bytes 1474560 | tf_op jit(solution)/shard_map/all_gather | solution.py:60
  233.2 3.7 copy-start.2
  240.8 1.3 copy-start
  242.1 44.4 %copy-start.7 = (bf16[2,64,4096]{2,1,0:T(8,128)(2,1)S(1)}, bf16[2,64,4096]{2,1,0:T(8,128)(2,1)}, u32[]{:S(2)}) copy-start(bf16[2,64,4096]{2,1,0:T(8,128)(2,1)} %param.7) | copy-start | bytes 3145732
  242.8 121.8 %all-reduce.10.cloned.1.call-start = ((), (), s32[]{:S(2)}) async-start(), calls=%async_computation.5 | async-start | bytes 524288 | tf_op jit(solution)/shard_map/psum | solution.py:78
  286.5 5.2 %copy-start.1 = (f32[128,4096]{1,0:T(8,128)S(1)}, f32[128,4096]{1,0:T(8,128)}, u32[]{:S(2)}) copy-start(f32[128,4096]{1,0:T(8,128)} %copy-done) | copy-start | bytes 6291460
  292.2 72.9 %copy-start.4 = (f32[64,4096]{1,0:T(8,128)}, f32[64,4096]{1,0:T(8,128)S(1)}, u32[]{:S(2)}) copy-start(f32[64,4096]{1,0:T(8,128)S(1)} %convolution_subtract_fusion.2) | copy-start | bytes 3145732
  293.9 0.7 copy-start.9
  294.6 103.8 %all-reduce.12.cloned.1.call-start = ((), (), s32[]{:S(2)}) async-start(), calls=%async_computation.6 | async-start | bytes 524288 | tf_op jit(solution)/shard_map/psum | solution.py:78
  364.6 96.5 %all-gather.11.cloned.1.call-start = ((), (), s32[]{:S(2)}) async-start(), calls=%async_computation.7 | async-start | bytes 5242880 | tf_op jit(solution)/shard_map/all_gather | solution.py:80
  461.1 3.7 copy-start.3
Sparse Core Ops, SparseCore 0:
  15.2 42.9 all-gather.4
  66.6 69.7 all-reduce.5
  138.7 31.5 all-reduce.7
  171.7 34.5 all-gather.6
  242.9 41.8 all-gather.8
  294.7 69.8 all-reduce.9
  366.9 31.4 all-reduce.11
  400.0 34.4 all-gather.10
